TPU v7x, 32 devices: a whole 2x2x4 slice. The times are simulated.
32 devices in a mesh: groups: 2 (over x), kv: 16 (over z, y, core).
Axes of the slice: x: 2, y: 2, z: 4, core: 2. Of those that a mesh axis runs over, the one named last changes fastest.
Arguments:
- queries: bfloat16 [80, 18432], P('groups', 'kv'), parts along dimension 0, may hold values from -240 to 240
- latent_cache: bfloat16 [80, 2048, 576], P('groups', 'kv'), parts along dimension 0, may hold values from -6 to 6
- context_lengths: int32 [80], P('groups'), parts along dimension 0, may hold values from 128 to 2048, as said below
- value_up: bfloat16 [16384, 128], P('kv'), may hold values from -0.25 to 0.25
- out_proj: bfloat16 [4096, 7168], P('kv'), may hold values from -0.09375 to 0.09375
- residual: bfloat16 [80, 7168], P('groups', 'kv'), parts along dimension 0, may hold values from -0.75 to 0.75
- norm_gain: bfloat16 [7168], P('kv'), may hold values from 0.5 to 1.5
- expert_ids: int32 [80, 8], P('groups'), parts along dimension 0, may hold values from 0 to 255, all different within a row; in each aligned block of 40 rows (0 to 39, 40 to 79, ...) at most 2 rows name the same one
- gate_weights: float32 [80, 8], P('groups'), parts along dimension 0, may hold values from 0.05 to 0.5
Outputs:
- dispatched: bfloat16 [512, 2, 7168], P(('groups', 'kv')), parts along dimension 0
- slot_scale: float32 [512, 2], P(('groups', 'kv')), parts along dimension 0
- slot_gate: float32 [512, 2], P(('groups', 'kv')), parts along dimension 0
There are 2 independent parts, one for each index of `groups`. A program takes and returns all parts, laid end to end along the dimension named above; an argument that names none is the same for every part. Nothing has to cross between parts.
Inputs may be any that keep to these rules, and one draw needn't show every extreme that they name: `context_lengths`: multiples of 128; some sequence is 2048 long. `expert_ids`: each token names 8 different experts; no expert is named by more than 2 tokens, a bound that some block reaches.
All inputs are finite; a program needn't handle non-finite values. Where the computation divides by a largest or mean magnitude, that divisor is 1e-20 or more.
Results may differ from a plain program's by a relative error of at most 0.0069.
Values may be sent and summed in bfloat16 or wider, within the bound.
A program may use at most 64 MiB of HBM per device.

v0:
```python
import jax
import jax.numpy as jnp
from jax import lax
from jax.sharding import PartitionSpec as P

H = 32
LAT = 512
ROPE = 64
VD = 128
D = 7168
EXPERTS = 256
TOPK = 8
CAP = 2
score_scale = 192.0 ** (-0.5)
masked_score = -1e30
small_eps = 1e-06


def from_partner(value, axis, bit):
    mask = 2**bit
    pairs = [(source, source ^ mask) for source in range(lax.axis_size(axis))]
    return lax.ppermute(value, axis, pairs)


def slot_targets(expert_ids):
    flat_ids = expert_ids.reshape(-1)
    order_index = jnp.arange(flat_ids.shape[0], dtype=jnp.int32)
    same_before = (flat_ids[:, None] == flat_ids[None, :]) & (
        order_index[None, :] < order_index[:, None]
    )
    rank_within = jnp.sum(same_before.astype(jnp.int32), axis=1)
    return flat_ids * CAP + rank_within


def slot_match(targets, first_slot, slot_count):
    slot_index = first_slot + jnp.arange(slot_count, dtype=jnp.int32)
    return (slot_index[:, None] == targets[None, :]).astype(jnp.float32)


def token_picker(matches, seq_count):
    return jnp.sum(matches.reshape(matches.shape[0], seq_count, TOPK), axis=2)


def per_device(
    queries,
    latent_cache,
    context_lengths,
    value_up,
    out_proj,
    residual,
    norm_gain,
    expert_ids,
    gate_weights,
):
    kv_count = lax.axis_size("kv")
    shard_index = lax.axis_index("kv")
    seq_count = queries.shape[0]
    query_rows = lax.all_gather(queries, "kv", axis=1, tiled=True).reshape(seq_count, H, LAT + ROPE)
    ctx_local = latent_cache.shape[1]
    scores = (
        jnp.einsum("shq,scq->shc", query_rows, latent_cache, preferred_element_type=jnp.float32)
        * score_scale
    )
    position = shard_index * ctx_local + jnp.arange(ctx_local, dtype=jnp.int32)
    valid_mask = (position[None, :] < context_lengths[:, None])[:, None, :]
    scores = jnp.where(valid_mask, scores, masked_score)
    local_max = jnp.max(scores, axis=2)
    weights = jnp.where(valid_mask, jnp.exp(scores - local_max[:, :, None]), 0.0)
    local_total = jnp.sum(weights, axis=2)
    local_out = jnp.einsum(
        "shc,scl->shl",
        weights.astype(jnp.bfloat16),
        latent_cache[:, :, :LAT],
        preferred_element_type=jnp.float32,
    )
    out_rows = out_proj.shape[0]
    col_count = H * LAT // kv_count
    segment = min(col_count, LAT)
    head_count = col_count // segment
    head_start = shard_index * col_count // LAT
    global_max = lax.pmax(local_max, "kv")
    scaling = jnp.exp(local_max - global_max)
    weight_total = lax.psum(local_total * scaling, "kv")
    scaled = (local_out * scaling[:, :, None]).reshape(seq_count, H * LAT)
    merged_sum = lax.psum_scatter(scaled, "kv", scatter_dimension=1, tiled=True).reshape(
        seq_count, head_count, segment
    )
    own_total = lax.dynamic_slice_in_dim(weight_total, head_start, head_count, 1)
    merged = merged_sum / own_total[:, :, None]
    projector = value_up.reshape(head_count, segment, VD).astype(jnp.float32)
    value_part = jnp.einsum("shl,hlv->shv", merged, projector, precision=lax.Precision.HIGHEST)
    holders = kv_count // H if kv_count > H else 1
    for bit in range(holders.bit_length() - 1):
        value_part = value_part + from_partner(value_part, "kv", bit)
    value_rows = value_part.astype(jnp.bfloat16).reshape(seq_count, head_count * VD)
    if holders > 1:
        value_rows = lax.dynamic_slice_in_dim(
            value_rows, shard_index % holders * out_rows, out_rows, 1
        )
    partial_out = jnp.dot(value_rows, out_proj, preferred_element_type=jnp.float32)
    experts_local = EXPERTS // kv_count
    slot_count = experts_local * CAP
    targets = slot_targets(expert_ids)
    own_match = slot_match(targets, shard_index * slot_count, slot_count)
    own_pick = token_picker(own_match, seq_count)
    slot_gate = jnp.dot(own_match, gate_weights.reshape(-1), precision=lax.Precision.HIGHEST)
    attn_rows = lax.psum(partial_out, "kv")
    resid_rows, gain_cols = (
        lax.all_gather(residual, "kv", axis=1, tiled=True),
        lax.all_gather(norm_gain, "kv", axis=0, tiled=True),
    )
    summed = attn_rows + resid_rows.astype(jnp.float32)
    inverse_rms = lax.rsqrt(jnp.mean(summed * summed, axis=1) + small_eps)
    normed = summed * inverse_rms[:, None] * gain_cols.astype(jnp.float32)
    peak_abs = jnp.max(jnp.abs(normed), axis=1) + small_eps
    coded_rows = (normed / peak_abs[:, None]).astype(jnp.bfloat16)
    dispatched = jnp.dot(
        own_pick.astype(jnp.bfloat16), coded_rows, preferred_element_type=jnp.float32
    ).astype(jnp.bfloat16)
    slot_scale = jnp.dot(own_pick, peak_abs, precision=lax.Precision.HIGHEST)
    return (
        dispatched.reshape(experts_local, CAP, D),
        slot_scale.reshape(experts_local, CAP),
        slot_gate.reshape(experts_local, CAP),
    )


def solution(mesh):
    in_specs = (
        P("groups", "kv"),
        P("groups", "kv", None),
        P("groups"),
        P("kv", None),
        P("kv", None),
        P("groups", "kv"),
        P("kv"),
        P("groups", None),
        P("groups", None),
    )
    out_specs = (
        P(("groups", "kv"), None, None),
        P(("groups", "kv"), None),
        P(("groups", "kv"), None),
    )
    return jax.shard_map(
        per_device, mesh=mesh, in_specs=in_specs, out_specs=out_specs, check_vma=False
    )
```

profile of v0, /device:TPU:0, one launch (start us, length us, event | category | flops | bytes accessed | tf_op | source)
XLA Modules:
  0.0 314.2 jit_solution(11004834008479304627)
XLA Ops:
  7.2 0.7 all-gather.3.cloned.1.call-update
  8.0 0.7 broadcast_compare_fusion.1
  8.7 43.6 %all-gather.3.cloned.1.call-done = bf16[40,18432]{1,0:T(8,128)(2,1)} async-done(((bf16[40,1152]{1,0:T(8,128)(2,1)}), bf16[40,18432]{1,0:T(8,128)(2,1)}) %all-gather.3.cloned.1.call-update) | async-done | bytes 1474576 | tf_op jit(solution)/shard_map/all_gather | solution.py:58
  52.3 3.3 %reshape.111 = bf16[40,32,576]{2,1,0:T(8,128)(2,1)S(1)} reshape(bf16[40,18432]{1,0:T(8,128)(2,1)} %all-gather.3.cloned.1.call-done) | data formatting | bytes 2949120 | tf_op jit(solution)/shard_map/reshape | solution.py:58
  55.5 3.9 %fusion.26 = (f32[40,32]{1,0:T(8,128)S(1)}, f32[40,32,128]{2,1,0:T(8,128)S(1)}) fusion(bf16[40,32,576]{2,1,0:T(8,128)(2,1)S(1)} %reshape.111, bf16[40,128,576]{1,2,0:T(8,128)(2,1)} %param.10, pred[40,128]{1,0:T(8,128)(4,1)S(1)} %broadcast_compare_fusion.1), kind=kOutput, calls=%fused_computation.47 | convolution fusion | flops 189233920 | bytes 8038400 | tf_op jit(solution)/shard_map/shq,scq->shc/dot_general | solution.py:61
  59.4 59.5 %pmax.7 = f32[40,32]{1,0:T(8,128)S(1)} all-reduce(f32[40,32]{1,0:T(8,128)S(1)} %get-tuple-element.5), channel_id=1, replica_groups=mesh['groups'=2,'kv'=16] {'kv'}, use_global_device_ids=true, to_apply=%region_3.4 | all-reduce | flops 1280 | bytes 10240 | tf_op jit(solution)/shard_map/pmax | solution.py:81
  118.9 0.4 fusion.7
  119.4 3.9 %fusion.2 = f32[40,32,512]{2,1,0:T(8,128)S(1)} fusion(bf16[40,128,576]{1,2,0:T(8,128)(2,1)} %param.10, f32[40,32]{1,0:T(8,128)S(1)} %get-tuple-element.4, f32[40,32,128]{2,1,0:T(8,128)S(1)} %get-tuple-element.6, f32[40,32]{1,0:T(8,128)S(1)} %get-tuple-element.5, pred[40,128]{1,0:T(8,128)(4,1)S(1)} %broadcast_compare_fusion.1), kind=kOutput, calls=%fused_computation.3 | convolution fusion | flops 168919040 | bytes 8535040 | tf_op jit(solution)/shard_map/shc,scl->shl/dot_general | solution.py:70
  123.3 3.0 copy.51
  126.4 0.6 copy-done.3
  127.2 0.2 convert_reduce_fusion
  127.4 0.1 reduce_sum.39
  127.6 19.1 %all-gather = bf16[16,448,40]{1,2,0:T(8,128)(2,1)S(1)} all-gather(bf16[1,448,40]{1,2,0:T(8,128)(2,1)S(1)} %bitcast.43), channel_id=1, replica_groups=mesh['groups'=2,'kv'=16] {'kv'}, dimensions={0}, use_global_device_ids=true | all-gather | bytes 609280 | tf_op jit(solution)/shard_map/all_gather | solution.py:109
  146.7 59.9 %psum.14 = f32[40,32]{1,0:T(8,128)S(1)} all-reduce(f32[40,32]{1,0:T(8,128)S(1)} %get-tuple-element.3), channel_id=1, replica_groups=mesh['groups'=2,'kv'=16] {'kv'}, use_global_device_ids=true, to_apply=%region_6.7 | all-reduce | flops 1280 | bytes 10240 | tf_op jit(solution)/shard_map/psum | solution.py:83
  206.7 1.1 reshape.113
  207.8 0.1 broadcast_divide_fusion
  207.9 0.2 fusion.6
  208.2 3.8 %fusion.17 = f32[40,7168]{1,0:T(8,128)} fusion(bf16[256,7168]{1,0:T(8,128)(2,1)} %param.13, bf16[2,5,8,128]{3,2,1,0:T(8,128)(2,1)S(1)} %fusion.6), kind=kOutput, calls=%fused_computation.28 | convolution fusion | flops 146800640 | bytes 4837376 | tf_op jit(solution)/shard_map/dot_general | solution.py:100
  212.1 0.2 copy.43
  212.3 0.5 reshape.125
  212.9 0.6 dynamic-slice
  214.2 0.3 dynamic-update-slice
  214.4 57.8 %all-reduce = bf16[7168]{0:T(1024)(128)(2,1)S(1)} all-reduce(bf16[7168]{0:T(1024)(128)(2,1)S(1)} %dynamic-update-slice), channel_id=1, replica_groups=mesh['groups'=2,'kv'=16] {'kv'}, use_global_device_ids=true, to_apply=%add | all-reduce | flops 7168 | bytes 28672
  272.4 0.1 convert_reduce_fusion.1
  272.6 0.1 broadcast_compare_fusion
  272.7 0.8 fusion.15
  273.5 30.1 %all-reduce.3.cloned.1.call-done = f32[40,7168]{1,0:T(8,128)} async-done(((f32[40,7168]{1,0:T(8,128)}), f32[40,7168]{1,0:T(8,128)}) %all-reduce.3.cloned.1.call-update) | async-done | bytes 1146896 | tf_op jit(solution)/shard_map/psum | solution.py:107
  303.6 1.6 multiply_reduce_fusion
  305.2 0.4 abs_reduce_fusion
  305.5 0.4 convolution_convert_fusion
  306.0 0.9 reshape.116
  306.9 0.8 fusion.20
  (35 shorter events, 0.8 us)
Async XLA Ops:
  7.2 200.8 %copy-start = (bf16[1024,128]{1,0:T(8,128)(2,1)S(1)}, bf16[1024,128]{1,0:T(8,128)(2,1)}, u32[]{:S(2)}) copy-start(bf16[1024,128]{1,0:T(8,128)(2,1)} %param.12) | copy-start | bytes 786436
  7.2 45.1 %all-gather.3.cloned.1.call-start = ((), (), s32[]{:S(2)}) async-start(), calls=%async_computation.1 | async-start | bytes 1566720 | tf_op jit(solution)/shard_map/all_gather | solution.py:58
  7.9 198.8 %reduce-scatter.2.cloned.1.call-start = ((), (), s32[]{:S(2)}) async-start(), calls=%async_computation.2 | async-start | bytes 2785280 | tf_op jit(solution)/shard_map/reduce_scatter | solution.py:85
  126.3 0.7 copy-start.3
  126.3 1.3 copy-start.2
  126.3 177.2 %all-reduce.3.cloned.1.call-start = ((), (), s32[]{:S(2)}) async-start(), calls=%async_computation.3 | async-start | bytes 2293760 | tf_op jit(solution)/shard_map/psum | solution.py:107
  212.3 0.7 copy-start.6
  212.3 1.9 copy-start.5
  212.3 60.0 %copy-start.4 = (f32[40,8]{0,1:T(8,128)S(1)}, f32[40,8]{0,1:T(8,128)}, u32[]{:S(2)}) copy-start(f32[40,8]{0,1:T(8,128)} %param.17) | copy-start | bytes 3844
  303.6 1.6 copy-start.1
Sparse Core Ops, SparseCore 0:
  10.2 42.0 all-gather.2
  126.5 61.4 reduce-scatter.1
  212.2 91.3 all-reduce.2
where the time goes:
time: 315 us; the launch traced here: 314 us
  blocking collectives  196 us (62%)
  waiting for transfers between devices  74.4 us (24%)
  between operations  14.6 us (5%)
  matrix products  13.9 us (4%)
  local copies, waits for them, and re-layouts  11.1 us (4%)
  other arithmetic  3.74 us (1%)
    psum x1, blocking collectives, per_device(): weight_total = lax.psum(local_total * scaling, 'kv')  59.9 us
    pmax x1, blocking collectives, per_device(): global_max = lax.pmax(local_max, 'kv')  59.5 us
    unnamed x1, blocking collectives  57.8 us
    all_gather x1, waiting for transfers between devices, per_device(): lax.all_gather(queries, 'kv', axis=1, tiled=True)  43.6 us
    psum x1, waiting for transfers between devices, per_device(): attn_rows = lax.psum(partial_out, 'kv')  30.1 us
    all_gather x1, blocking collectives, per_device(): lax.all_gather(residual, 'kv', axis=1, tiled=True)  19.1 us
  transfers between devices with their start and end apart: 3, of which 2 were waited for; matrix products, arithmetic and copies ran while one was open for 1% of the time, Pallas kernels for 0%

commit v1 on v0

--- a/solution.py
+++ b/solution.py
@@ -80,7 +80,7 @@
     head_start = shard_index * col_count // LAT
     global_max = lax.pmax(local_max, "kv")
     scaling = jnp.exp(local_max - global_max)
-    weight_total = lax.psum(local_total * scaling, "kv")
+    weight_total = jnp.sum(lax.all_gather(local_total * scaling, "kv"), 0)
     scaled = (local_out * scaling[:, :, None]).reshape(seq_count, H * LAT)
     merged_sum = lax.psum_scatter(scaled, "kv", scatter_dimension=1, tiled=True).reshape(
         seq_count, head_count, segment

time: 315 us -> 299 us (0.949)
  blocking collectives: 196 us -> 157 us
  waiting for transfers between devices: 74.4 us -> 97.8 us
    psum x1 -> x0, blocking collectives: 59.9 us -> none  [per_device(): weight_total = lax.psum(local_total * scaling, 'kv')]
    reduce_scatter x1, waiting for transfers between devices: 0.01 us -> 22.3 us  [per_device(): lax.psum_scatter(scaled, 'kv', scatter_dimension=1, tiled=True)]
    all_gather x0 -> x1, blocking collectives: none -> 20 us  [per_device(): weight_total = jnp.sum(lax.all_gather(local_total * scaling, 'kv'), 0)]
  transfers between devices with their start and end apart: 3 -> 3, of which waited for: 2 -> 3; matrix products, arithmetic and copies ran while one was open for 1% -> 1% of each run, Pallas kernels for 0% -> 0%
where the time goes in v1:
time: 299 us; the launch traced here: 298 us
  blocking collectives  157 us (53%)
  waiting for transfers between devices  97.8 us (33%)
  between operations  14.6 us (5%)
  matrix products  13.9 us (5%)
  local copies, waits for them, and re-layouts  11.2 us (4%)
  other arithmetic  3.76 us (1%)
    pmax x1, blocking collectives, per_device(): global_max = lax.pmax(local_max, 'kv')  59.5 us
    unnamed x1, blocking collectives  58.2 us
    all_gather x1, waiting for transfers between devices, per_device(): lax.all_gather(queries, 'kv', axis=1, tiled=True)  43.6 us
    psum x1, waiting for transfers between devices, per_device(): attn_rows = lax.psum(partial_out, 'kv')  31.2 us
    reduce_scatter x1, waiting for transfers between devices, per_device(): lax.psum_scatter(scaled, 'kv', scatter_dimension=1, tiled=True)  22.3 us
    all_gather x1, blocking collectives, per_device(): weight_total = jnp.sum(lax.all_gather(local_total * scaling, 'kv'), 0)  20 us
    all_gather x1, blocking collectives, per_device(): lax.all_gather(residual, 'kv', axis=1, tiled=True)  19.1 us
  transfers between devices with their start and end apart: 3, of which 3 were waited for; matrix products, arithmetic and copies ran while one was open for 1% of the time, Pallas kernels for 0%

profile of v1, /device:TPU:0, one launch (start us, length us, event | category | flops | bytes accessed | tf_op | source)
XLA Modules:
  0.0 298.3 jit_solution(17798542982016087512)
XLA Ops:
  7.2 0.7 all-gather.5.cloned.1.call-update
  8.0 0.7 broadcast_compare_fusion.1
  8.7 43.6 %all-gather.5.cloned.1.call-done = bf16[40,18432]{1,0:T(8,128)(2,1)} async-done(((bf16[40,1152]{1,0:T(8,128)(2,1)}), bf16[40,18432]{1,0:T(8,128)(2,1)}) %all-gather.5.cloned.1.call-update) | async-done | bytes 1474576 | tf_op jit(solution)/shard_map/all_gather | solution.py:58
  52.3 3.3 %reshape.111 = bf16[40,32,576]{2,1,0:T(8,128)(2,1)S(1)} reshape(bf16[40,18432]{1,0:T(8,128)(2,1)} %all-gather.5.cloned.1.call-done) | data formatting | bytes 2949120 | tf_op jit(solution)/shard_map/reshape | solution.py:58
  55.5 3.9 %fusion.25 = (f32[40,32]{1,0:T(8,128)S(1)}, f32[40,32,128]{2,1,0:T(8,128)S(1)}) fusion(bf16[40,32,576]{2,1,0:T(8,128)(2,1)S(1)} %reshape.111, bf16[40,128,576]{1,2,0:T(8,128)(2,1)} %param.10, pred[40,128]{1,0:T(8,128)(4,1)S(1)} %broadcast_compare_fusion.1), kind=kOutput, calls=%fused_computation.47 | convolution fusion | flops 189233920 | bytes 8038400 | tf_op jit(solution)/shard_map/shq,scq->shc/dot_general | solution.py:61
  59.4 59.5 %pmax.7 = f32[40,32]{1,0:T(8,128)S(1)} all-reduce(f32[40,32]{1,0:T(8,128)S(1)} %get-tuple-element.5), channel_id=1, replica_groups=mesh['groups'=2,'kv'=16] {'kv'}, use_global_device_ids=true, to_apply=%region_3.4 | all-reduce | flops 1280 | bytes 10240 | tf_op jit(solution)/shard_map/pmax | solution.py:81
  118.9 0.4 fusion.7
  119.4 3.9 %fusion.2 = f32[40,32,512]{2,1,0:T(8,128)S(1)} fusion(bf16[40,128,576]{1,2,0:T(8,128)(2,1)} %param.10, f32[40,32]{1,0:T(8,128)S(1)} %get-tuple-element.4, f32[40,32,128]{2,1,0:T(8,128)S(1)} %get-tuple-element.6, f32[40,32]{1,0:T(8,128)S(1)} %get-tuple-element.5, pred[40,128]{1,0:T(8,128)(4,1)S(1)} %broadcast_compare_fusion.1), kind=kOutput, calls=%fused_computation.3 | convolution fusion | flops 168919040 | bytes 8535040 | tf_op jit(solution)/shard_map/shc,scl->shl/dot_general | solution.py:70
  123.3 3.0 %copy.65 = f32[5,8,32,512]{3,1,2,0:T(8,128)} copy(f32[5,8,32,512]{3,2,1,0:T(8,128)S(1)} %bitcast.42) | data formatting | bytes 5242880
  126.4 0.6 copy-done.3
  127.2 0.2 convert_reduce_fusion
  127.6 19.1 %all-gather.2 = bf16[16,448,40]{1,2,0:T(8,128)(2,1)S(1)} all-gather(bf16[1,448,40]{1,2,0:T(8,128)(2,1)S(1)} %bitcast.45), channel_id=1, replica_groups=mesh['groups'=2,'kv'=16] {'kv'}, dimensions={0}, use_global_device_ids=true | all-gather | bytes 609280 | tf_op jit(solution)/shard_map/all_gather | solution.py:109
  146.8 20.0 %all-gather.1 = f32[16,40,32]{1,2,0:T(8,128)S(1)} all-gather(f32[1,40,32]{1,2,0:T(8,128)S(1)} %copy.53), channel_id=2, replica_groups=mesh['groups'=2,'kv'=16] {'kv'}, dimensions={0}, use_global_device_ids=true | all-gather | bytes 87040 | tf_op jit(solution)/shard_map/all_gather | solution.py:83
  166.9 22.3 %reduce-scatter.2.cloned.1.call-done = f32[40,1024]{1,0:T(8,128)} async-done(((f32[40,16384]{1,0:T(8,128)}), f32[40,1024]{1,0:T(8,128)}) %reduce-scatter.2.cloned.1.call-update) | async-done | bytes 163856 | tf_op jit(solution)/shard_map/reduce_scatter | solution.py:85
  189.2 1.1 reshape.113
  190.3 0.1 broadcast_divide_fusion
  190.4 0.2 fusion.6
  190.7 3.8 %fusion.17 = f32[40,7168]{1,0:T(8,128)} fusion(bf16[256,7168]{1,0:T(8,128)(2,1)} %param.13, bf16[2,5,8,128]{3,2,1,0:T(8,128)(2,1)S(1)} %fusion.6), kind=kOutput, calls=%fused_computation.28 | convolution fusion | flops 146800640 | bytes 4837376 | tf_op jit(solution)/shard_map/dot_general | solution.py:100
  194.6 0.2 copy.57
  194.8 0.5 reshape.129
  195.4 0.6 dynamic-slice
  196.7 0.3 dynamic-update-slice
  197.0 58.2 %all-reduce = bf16[7168]{0:T(1024)(128)(2,1)S(1)} all-reduce(bf16[7168]{0:T(1024)(128)(2,1)S(1)} %dynamic-update-slice), channel_id=1, replica_groups=mesh['groups'=2,'kv'=16] {'kv'}, use_global_device_ids=true, to_apply=%add | all-reduce | flops 7168 | bytes 28672
  255.4 0.1 convert_reduce_fusion.1
  255.5 0.1 broadcast_compare_fusion
  255.6 0.8 fusion.15
  256.4 31.2 %all-reduce.3.cloned.1.call-done = f32[40,7168]{1,0:T(8,128)} async-done(((f32[40,7168]{1,0:T(8,128)}), f32[40,7168]{1,0:T(8,128)}) %all-reduce.3.cloned.1.call-update) | async-done | bytes 1146896 | tf_op jit(solution)/shard_map/psum | solution.py:107
  287.6 1.6 multiply_reduce_fusion
  289.2 0.4 abs_reduce_fusion
  289.6 0.4 convolution_convert_fusion
  290.0 0.9 reshape.116
  291.0 0.8 fusion.20
  (38 shorter events, 1.0 us)
Async XLA Ops:
  7.2 183.3 %copy-start = (bf16[1024,128]{1,0:T(8,128)(2,1)S(1)}, bf16[1024,128]{1,0:T(8,128)(2,1)}, u32[]{:S(2)}) copy-start(bf16[1024,128]{1,0:T(8,128)(2,1)} %param.12) | copy-start | bytes 786436
  7.2 45.1 %all-gather.5.cloned.1.call-start = ((), (), s32[]{:S(2)}) async-start(), calls=%async_computation.1 | async-start | bytes 1566720 | tf_op jit(solution)/shard_map/all_gather | solution.py:58
  7.9 181.3 %reduce-scatter.2.cloned.1.call-start = ((), (), s32[]{:S(2)}) async-start(), calls=%async_computation.2 | async-start | bytes 2785280 | tf_op jit(solution)/shard_map/reduce_scatter | solution.py:85
  126.3 0.7 copy-start.3
  126.3 1.3 copy-start.2
  126.3 161.3 %all-reduce.3.cloned.1.call-start = ((), (), s32[]{:S(2)}) async-start(), calls=%async_computation.3 | async-start | bytes 2293760 | tf_op jit(solution)/shard_map/psum | solution.py:107
  194.8 0.7 copy-start.6
  194.8 1.9 copy-start.5
  194.8 60.4 %copy-start.4 = (f32[40,8]{0,1:T(8,128)S(1)}, f32[40,8]{0,1:T(8,128)}, u32[]{:S(2)}) copy-start(f32[40,8]{0,1:T(8,128)} %param.17) | copy-start | bytes 3844
  287.6 1.6 copy-start.1
Sparse Core Ops, SparseCore 0:
  10.2 42.0 all-gather.4
  126.5 62.7 reduce-scatter.1
  194.7 92.9 all-reduce.2
